TPU v7x, 512 devices: a 4x2x32 block of a 4x8x32 slice. The times are simulated.
512 devices in a mesh: slide: 2 (over y), row: 64 (over z, core), col: 4 (over x).
Axes of the slice: x: 4, y: 2, z: 32, core: 2. Of those that a mesh axis runs over, the one named last changes fastest.
The devices are a block of a 4x8x32 slice.
Arguments:
- features: bfloat16 [896, 1792, 96], P(('slide', 'row'), 'col'), parts along dimension 0, may hold values from -6 to 6
- region_ids: int32 [128, 256, 49], P(('slide', 'row'), 'col'), parts along dimension 0, may hold values from 0 to 1073741823, as said below
- qkv_weight: bfloat16 [96, 288], replicated, may hold values from -0.625 to 0.625
- proj_weight: bfloat16 [96, 96], replicated, may hold values from -0.625 to 0.625
- rel_bias: float32 [169, 3], replicated, may hold values from -5 to 280
- fc1_weight: bfloat16 [96, 384], replicated, may hold values from -0.625 to 0.625
- fc2_weight: bfloat16 [384, 96], replicated, may hold values from -0.3125 to 0.3125
Outputs:
- block_out: bfloat16 [896, 1792, 96], P(('slide', 'row'), 'col'), parts along dimension 0
There are 2 independent parts, one for each index of `slide`. A program takes and returns all parts, laid end to end along the dimension named above; an argument that names none is the same for every part. Nothing has to cross between parts.
Inputs may be any that keep to these rules, and one draw needn't show every extreme that they name: `region_ids`: within each window, each token's id marks the region it belongs to; a window holds at most 4 distinct ids.
All inputs are finite; a program needn't handle non-finite values.
Results may differ from a plain program's by a relative error of at most 0.011.
Values may be sent and summed in bfloat16 or wider, within the bound.
No kernel may reach another device: no remote copies, remote signals or barrier semaphores. Data moves between devices by JAX's collectives and lax.ppermute only.
A program may use at most 64 MiB of HBM per device.

v0:
```python
import jax
import jax.numpy as jnp
import numpy as np
from jax import lax
from jax.sharding import PartitionSpec as P

HEADS = 3
WIN = 7
SHIFT = 3


epsilon = 1e-05


def shifted_2(value, axis, steps):
    count = lax.axis_size(axis)
    pairs = [(source, (source + steps) % count) for source in range(count)]
    return lax.ppermute(value, axis, pairs)


def layer_norm(values):
    average = jnp.mean(values, axis=-1, keepdims=True)
    centred = values - average
    variance = jnp.mean(centred * centred, axis=-1, keepdims=True)
    return centred * lax.rsqrt(variance + epsilon)


def relative_onehot():
    positions = np.arange(WIN * WIN)
    row_of = positions // WIN
    col_of = positions % WIN
    index = (row_of[:, None] - row_of[None, :] + WIN - 1) * (2 * WIN - 1) + (
        col_of[:, None] - col_of[None, :] + WIN - 1
    )
    table = np.zeros((WIN**4, (2 * WIN - 1) ** 2), np.float32)
    table[np.arange(WIN**4), index.reshape(-1)] = 1.0
    return table


def window_attention(normed_tile, window_ids, qkv_weight, proj_weight, pos_bias):
    tile_rows, tile_cols, width = normed_tile.shape
    win_rows = tile_rows // WIN
    win_cols = tile_cols // WIN
    window_count = win_rows * win_cols
    head_dim = width // HEADS
    windows = (
        normed_tile.reshape(win_rows, WIN, win_cols, WIN, width)
        .transpose(0, 2, 1, 3, 4)
        .reshape(window_count * WIN * WIN, width)
    )
    projected = jnp.dot(windows, qkv_weight, preferred_element_type=jnp.float32).astype(
        jnp.bfloat16
    )
    projected = projected.reshape(window_count, WIN * WIN, 3, HEADS, head_dim)
    queries = projected[:, :, 0]
    key_rows = projected[:, :, 1]
    value_rows = projected[:, :, 2]
    scores = (
        jnp.einsum("wihd,wjhd->whij", queries, key_rows, preferred_element_type=jnp.float32)
        * head_dim ** (-0.5)
        + pos_bias[None]
    )
    flat_ids = window_ids.reshape(window_count, WIN * WIN)
    allowed = flat_ids[:, None, :, None] == flat_ids[:, None, None, :]
    scores = jnp.where(allowed, scores, -jnp.inf)
    weights = jax.nn.softmax(scores, axis=-1).astype(jnp.bfloat16)
    context = jnp.einsum(
        "whij,wjhd->wihd", weights, value_rows, preferred_element_type=jnp.float32
    ).astype(jnp.bfloat16)
    context = context.reshape(window_count * WIN * WIN, width)
    result = jnp.dot(context, proj_weight, preferred_element_type=jnp.float32).astype(jnp.bfloat16)
    return (
        result.reshape(win_rows, win_cols, WIN, WIN, width)
        .transpose(0, 2, 1, 3, 4)
        .reshape(tile_rows, tile_cols, width)
    )


def shards(features, region_ids, qkv_weight, proj_weight, rel_bias, fc1_weight, fc2_weight):
    tile_rows, tile_cols, width = features.shape
    pos_bias = jnp.dot(jnp.asarray(relative_onehot()), rel_bias, precision=lax.Precision.HIGHEST)
    pos_bias = pos_bias.reshape(WIN * WIN, WIN * WIN, HEADS).transpose(2, 0, 1)
    normed = layer_norm(features.astype(jnp.float32)).astype(jnp.bfloat16)
    strip_below = shifted_2(normed[:SHIFT], "row", -1)
    taller = jnp.concatenate([normed, strip_below], axis=0)
    strip_beside = shifted_2(taller[:, :SHIFT], "col", -1)
    wider = jnp.concatenate([taller, strip_beside], axis=1)
    shifted = wider[SHIFT:, SHIFT:]
    branch = window_attention(shifted, region_ids, qkv_weight, proj_weight, pos_bias)
    strip_above = shifted_2(branch[-SHIFT:], "row", 1)
    taller_back = jnp.concatenate([strip_above, branch], axis=0)
    strip_left = shifted_2(taller_back[:, -SHIFT:], "col", 1)
    wider_back = jnp.concatenate([strip_left, taller_back], axis=1)
    attended = wider_back[:tile_rows, :tile_cols]
    residual_sum = features.astype(jnp.float32) + attended.astype(jnp.float32)
    residual_sum = residual_sum.reshape(tile_rows * tile_cols, width)
    normed_two = layer_norm(residual_sum).astype(jnp.bfloat16)
    hidden = jax.nn.gelu(
        jnp.dot(normed_two, fc1_weight, preferred_element_type=jnp.float32), approximate=False
    ).astype(jnp.bfloat16)
    result = (
        residual_sum + jnp.dot(hidden, fc2_weight, preferred_element_type=jnp.float32)
    ).astype(jnp.bfloat16)
    return result.reshape(tile_rows, tile_cols, width)


def solution(mesh):
    return jax.shard_map(
        shards,
        mesh=mesh,
        in_specs=(
            P(("slide", "row"), "col", None),
            P(("slide", "row"), "col", None),
            P(),
            P(),
            P(),
            P(),
            P(),
        ),
        out_specs=P(("slide", "row"), "col", None),
        check_vma=False,
    )
```

profile of v0, /device:TPU:40, one launch (start us, length us, event | category | flops | bytes accessed | tf_op | source)
XLA Modules:
  0.0 124.5 jit_solution(1282985146748935979)
XLA Ops:
  0.0 1.5 %copy.20 = bf16[7,448,96]{2,1,0:T(8,128)(2,1)S(1)} copy(bf16[7,448,96]{1,2,0:T(8,128)(2,1)} %param.8) | data formatting | bytes 1204224 | tf_op args[0]
  1.9 1.0 fusion.21
  2.9 1.0 fusion.22
  4.0 43.0 %collective-permute-start = (bf16[3,448,96]{2,1,0:T(8,128)(2,1)S(1)}, bf16[3,448,96]{2,1,0:T(8,128)(2,1)S(1)}, u32[]{:S(2)}, u32[]{:S(2)}) collective-permute-start(bf16[3,448,96]{2,1,0:T(8,128)(2,1)S(1)} %slice.40), channel_id=1, source_target_pairs={{0,252},{4,0},{8,4},{12,8},{16,12},{20,16},{24,20},{28,24},{32,28}... | collective-permute-start | bytes 774152 | tf_op jit(solution)/shard_map/ppermute | solution.py:18
  47.0 3.9 %fusion.64 = f32[2401,3]{0,1:T(4,128)S(1)} fusion(f32[2401,169]{1,0:T(8,128)} %constant.78.clone, f32[169,3]{0,1:T(4,128)S(1)} %copy-done.5), kind=kOutput, calls=%fused_computation.96 | convolution fusion | flops 14607684 | bytes 1653916 | tf_op jit(solution)/shard_map/dot_general | solution.py:81
  50.9 0.8 collective-permute-done
  51.7 5.1 %collective-permute-start.1 = (bf16[10,3,96]{2,1,0:T(4,128)(2,1)S(1)}, bf16[10,3,96]{2,1,0:T(4,128)(2,1)S(1)}, u32[]{:S(2)}, u32[]{:S(2)}) collective-permute-start(bf16[10,3,96]{2,1,0:T(4,128)(2,1)S(1)} %pad_maximum_fusion.3), channel_id=1, source_target_pairs={{0,3},{1,0},{2,1},{3,2},{4,7},{5,4},{6,5},{7,6},{8,11},{9,8},{10,9... | collective-permute-start | bytes 17288 | tf_op jit(solution)/shard_map/ppermute | solution.py:18
  56.8 1.3 %broadcast_compare_fusion = pred[64,49,49]{1,2,0:T(8,128)(4,1)} fusion(s32[64,49]{1,0:T(8,128)S(1)} %bitcast.40), kind=kLoop, calls=%fused_computation.48 | loop fusion | flops 153664 | bytes 166208 | tf_op jit(solution)/shard_map/eq | solution.py:64
  58.3 0.7 copy.27
  60.1 0.7 convolution_convert_fusion
  60.8 14.6 %reshape.85 = bf16[64,49,3,3,32]{1,0,4,3,2:T(8,128)(2,1)} reshape(bf16[3136,288]{0,1:T(8,128)(2,1)S(1)} %convolution_convert_fusion) | data formatting | bytes 3612672 | tf_op jit(solution)/shard_map/reshape | solution.py:54
  75.4 3.4 %fusion.62 = (bf16[64,49,1,3,32]{1,0,4,3,2:T(8,128)(2,1)S(1)}, bf16[64,49,1,3,32]{1,0,4,3,2:T(8,128)(2,1)S(1)}, bf16[64,49,1,3,32]{1,0,4,3,2:T(8,128)(2,1)S(1)}) fusion(bf16[64,49,3,3,32]{1,0,4,3,2:T(8,128)(2,1)} %reshape.85), kind=kLoop, calls=%fused_computation.94 | loop fusion | bytes 3612672 | tf_op jit(solution)/shard_map/slice | solution.py:57
  78.9 3.5 %fusion.23 = f32[64,3,49,49]{2,3,1,0:T(8,128)S(1)} fusion(bf16[64,49,1,3,32]{1,0,4,3,2:T(8,128)(2,1)S(1)} %get-tuple-element.9, bf16[64,49,1,3,32]{1,0,4,3,2:T(8,128)(2,1)S(1)} %get-tuple-element.8), kind=kOutput, calls=%fused_computation.43 | convolution fusion | flops 29503488 | bytes 3048192 | tf_op jit(solution)/shard_map/wihd,wjhd->whij/dot_general | solution.py:59
  82.4 2.1 %fusion.63 = (f32[64,3,49]{2,1,0:T(4,128)S(1)}, f32[64,3,49,49]{2,3,1,0:T(8,128)S(1)}) fusion(f32[64,3,49,49]{2,3,1,0:T(8,128)S(1)} %fusion.23, f32[3,49,49]{1,2,0:T(8,128)S(1)} %bitcast.41, pred[64,49,49]{1,2,0:T(8,128)(4,1)S(1)} %copy-done.1), kind=kOutput, calls=%fused_computation.95 | output fusion | flops 3687984 | bytes 3908044 | tf_op jit(solution)/shard_map/sub | solution.py:66
  84.5 2.2 %fusion.24 = bf16[64,49,3,32]{1,3,2,0:T(8,128)(2,1)S(1)} fusion(f32[64,3,49,49]{2,3,1,0:T(8,128)S(1)} %get-tuple-element.11, f32[64,3,49]{2,1,0:T(4,128)S(1)} %get-tuple-element.10, bf16[64,49,1,3,32]{1,0,4,3,2:T(8,128)(2,1)S(1)} %get-tuple-element.7), kind=kOutput, calls=%fused_computation.46 | convolution fusion | flops 30726528 | bytes 3085824 | tf_op jit(solution)/shard_map/whij,wjhd->wihd/dot_general | solution.py:67
  87.3 2.1 %reshape.87 = bf16[3136,96]{0,1:T(8,128)(2,1)S(1)} reshape(bf16[64,49,3,32]{1,0,3,2:T(8,128)(2,1)S(1)} %copy.29) | data formatting | bytes 1204224 | tf_op jit(solution)/shard_map/reshape | solution.py:70
  91.5 7.3 %collective-permute-done.2 = bf16[3,448,96]{2,1,0:T(8,128)(2,1)S(1)} collective-permute-done((bf16[3,448,96]{2,1,0:T(8,128)(2,1)S(1)}, bf16[3,448,96]{2,1,0:T(8,128)(2,1)S(1)}, u32[]{:S(2)}, u32[]{:S(2)}) %collective-permute-start.2) | collective-permute-done | bytes 258080 | tf_op jit(solution)/shard_map/ppermute | solution.py:18
  99.0 2.2 %collective-permute-start.3 = (bf16[10,3,96]{2,1,0:T(4,128)(2,1)S(1)}, bf16[10,3,96]{2,1,0:T(4,128)(2,1)S(1)}, u32[]{:S(2)}, u32[]{:S(2)}) collective-permute-start(bf16[10,3,96]{2,1,0:T(4,128)(2,1)S(1)} %slice.45), channel_id=1, source_target_pairs={{0,1},{1,2},{2,3},{3,0},{4,5},{5,6},{6,7},{7,4},{8,9},{9,10},{10,1... | collective-permute-start | bytes 17288 | tf_op jit(solution)/shard_map/ppermute | solution.py:18
  101.2 4.6 %collective-permute-done.3 = bf16[10,3,96]{2,1,0:T(4,128)(2,1)S(1)} collective-permute-done((bf16[10,3,96]{2,1,0:T(4,128)(2,1)S(1)}, bf16[10,3,96]{2,1,0:T(4,128)(2,1)S(1)}, u32[]{:S(2)}, u32[]{:S(2)}) %collective-permute-start.3) | collective-permute-done | bytes 5792 | tf_op jit(solution)/shard_map/ppermute | solution.py:18
  106.5 1.0 multiply_reduce_fusion
  107.5 1.5 %copy.36 = f32[3136,96]{0,1:T(8,128)} copy(f32[3136,96]{1,0:T(8,128)S(1)} %bitcast.36) | data formatting | bytes 2408448 | tf_op jit(solution)/shard_map/reshape | solution.py:96
  109.1 13.4 %fusion.11 = bf16[3136,96]{0,1:T(8,128)(2,1)S(1)} fusion(f32[3136,96]{0,1:T(8,128)} %copy.36, bf16[384,96]{0,1:T(8,128)(2,1)S(1)} %copy-done.6, bf16[96,384]{1,0:T(8,128)(2,1)S(1)} %copy-done.7, f32[3136]{0:T(1024)S(1)} %rsqrt.21, f32[3136]{0:T(1024)S(1)} %div.27), kind=kOutput, calls=%fused_computation.25 | convolution fusion | flops 542201856 | bytes 1978880 | tf_op jit(solution)/shard_map/dot_general | solution.py:102
  122.4 1.0 reshape.91
  123.5 1.1 copy.34
  (46 shorter events, 5.2 us)
Async XLA Ops:
  0.0 60.1 %copy-start = (bf16[96,288]{1,0:T(8,128)(2,1)S(1)}, bf16[96,288]{1,0:T(8,128)(2,1)}, u32[]{:S(2)}) copy-start(bf16[96,288]{1,0:T(8,128)(2,1)} %param.10) | copy-start | bytes 165892
  0.0 46.9 %copy-start.3 = (s32[1,64,49]{1,0,2:T(1,128)S(1)}, s32[1,64,49]{1,0,2:T(1,128)}, u32[]{:S(2)}) copy-start(s32[1,64,49]{1,0,2:T(1,128)} %param.9) | copy-start | bytes 37636
  0.0 47.0 %copy-start.5 = (f32[169,3]{0,1:T(4,128)S(1)}, f32[169,3]{0,1:T(4,128)}, u32[]{:S(2)}) copy-start(f32[169,3]{0,1:T(4,128)} %param.12) | copy-start | bytes 6088
  4.0 47.7 %collective-permute-start = (bf16[3,448,96]{2,1,0:T(8,128)(2,1)S(1)}, bf16[3,448,96]{2,1,0:T(8,128)(2,1)S(1)}, u32[]{:S(2)}, u32[]{:S(2)}) collective-permute-start(bf16[3,448,96]{2,1,0:T(8,128)(2,1)S(1)} %slice.40), channel_id=1, source_target_pairs={{0,252},{4,0},{8,4},{12,8},{16,12},{20,16},{24,20},{28,24},{32,28}... | collective-permute-start | bytes 774152 | tf_op jit(solution)/shard_map/ppermute | solution.py:18
  51.7 7.3 %collective-permute-start.1 = (bf16[10,3,96]{2,1,0:T(4,128)(2,1)S(1)}, bf16[10,3,96]{2,1,0:T(4,128)(2,1)S(1)}, u32[]{:S(2)}, u32[]{:S(2)}) collective-permute-start(bf16[10,3,96]{2,1,0:T(4,128)(2,1)S(1)} %pad_maximum_fusion.3), channel_id=1, source_target_pairs={{0,3},{1,0},{2,1},{3,2},{4,7},{5,4},{6,5},{7,6},{8,11},{9,8},{10,9... | collective-permute-start | bytes 17288 | tf_op jit(solution)/shard_map/ppermute | solution.py:18
  78.9 3.5 %copy-start.1 = (pred[64,49,49]{1,2,0:T(8,128)(4,1)S(1)}, pred[64,49,49]{1,2,0:T(8,128)(4,1)}, u32[]{:S(2)}) copy-start(pred[64,49,49]{1,2,0:T(8,128)(4,1)} %broadcast_compare_fusion) | copy-start | bytes 460996
  78.9 3.5 %copy-start.2 = (f32[49,49,3]{0,1,2:T(8,128)S(1)}, f32[49,49,3]{0,1,2:T(8,128)}, u32[]{:S(2)}) copy-start(f32[49,49,3]{0,1,2:T(8,128)} %copy.27) | copy-start | bytes 86440
  86.7 2.8 %copy-start.4 = (bf16[96,96]{1,0:T(8,128)(2,1)S(1)}, bf16[96,96]{1,0:T(8,128)(2,1)}, u32[]{:S(2)}) copy-start(bf16[96,96]{1,0:T(8,128)(2,1)} %param.11) | copy-start | bytes 55300
  90.9 7.9 %collective-permute-start.2 = (bf16[3,448,96]{2,1,0:T(8,128)(2,1)S(1)}, bf16[3,448,96]{2,1,0:T(8,128)(2,1)S(1)}, u32[]{:S(2)}, u32[]{:S(2)}) collective-permute-start(bf16[3,448,96]{2,1,0:T(8,128)(2,1)S(1)} %slice.37), channel_id=1, source_target_pairs={{0,4},{4,8},{8,12},{12,16},{16,20},{20,24},{24,28},{28,32},{32,36}... | collective-permute-start | bytes 774152 | tf_op jit(solution)/shard_map/ppermute | solution.py:18
  98.8 10.2 %copy-start.6 = (bf16[384,96]{0,1:T(8,128)(2,1)S(1)}, bf16[384,96]{0,1:T(8,128)(2,1)}, u32[]{:S(2)}) copy-start(bf16[384,96]{0,1:T(8,128)(2,1)} %param.14) | copy-start | bytes 221188
  98.9 10.2 %copy-start.7 = (bf16[96,384]{1,0:T(8,128)(2,1)S(1)}, bf16[96,384]{1,0:T(8,128)(2,1)}, u32[]{:S(2)}) copy-start(bf16[96,384]{1,0:T(8,128)(2,1)} %param.13) | copy-start | bytes 221188
  99.0 6.8 %collective-permute-start.3 = (bf16[10,3,96]{2,1,0:T(4,128)(2,1)S(1)}, bf16[10,3,96]{2,1,0:T(4,128)(2,1)S(1)}, u32[]{:S(2)}, u32[]{:S(2)}) collective-permute-start(bf16[10,3,96]{2,1,0:T(4,128)(2,1)S(1)} %slice.45), channel_id=1, source_target_pairs={{0,1},{1,2},{2,3},{3,0},{4,5},{5,6},{6,7},{7,4},{8,9},{9,10},{10,1... | collective-permute-start | bytes 17288 | tf_op jit(solution)/shard_map/ppermute | solution.py:18
where the time goes:
time: 125 us
  starting transfers between devices  50.3 us (40%)
  local copies, waits for them, and re-layouts  29.6 us (24%)
  matrix products  23.9 us (19%)
  waiting for transfers between devices  12.8 us (10%)
  other arithmetic  7.66 us (6%)
    ppermute x4, starting transfers between devices, shifted_2(): return lax.ppermute(value, axis, pairs)  50.3 us
    reshape x1, local copies, waits for them, and re-layouts, window_attention(): projected = projected.reshape(window_count, WIN * WIN, 3, HEADS, head_dim)  14.6 us
    dot_general x1, matrix products, shards(): jnp.dot(hidden, fc2_weight, preferred_element_type=jnp.float32)  13.4 us
    ppermute x4, waiting for transfers between devices, shifted_2(): return lax.ppermute(value, axis, pairs)  12.8 us
    dot_general x1, matrix products, shards(): jnp.dot(jnp.asarray(relative_onehot()), rel_bias, precision=lax.Precision...  3.86 us
    dot_general x1, matrix products, window_attention(): jnp.einsum('wihd,wjhd->whij', queries, key_rows, preferred_element_type=j...  3.47 us
    slice x1, local copies, waits for them, and re-layouts, window_attention(): value_rows = projected[:, :, 2]  3.45 us
  transfers between devices with their start and end apart: 4, of which 3 were waited for; matrix products, arithmetic and copies ran while one was open for 5% of the time, Pallas kernels for 0%

commit v1 on v0

v1 whole, which is shorter than its diff:
```python
import functools

import jax
import jax.numpy as jnp
import numpy as np
from jax import lax
from jax.experimental import pallas as pl
from jax.experimental.pallas import tpu as pltpu
from jax.sharding import PartitionSpec as P

HEADS = 3
WIN = 7
SHIFT = 3
KEEP = WIN - SHIFT
PAD = 8
KEYS = WIN * PAD
GROUP = 5
LANES = 128
NEG = -1e30
F32 = jnp.float32
BF16 = jnp.bfloat16

epsilon = 1e-05


def moved(value, axis, steps):
    count = lax.axis_size(axis)
    pairs = [(source, (source + steps) % count) for source in range(count)]
    return lax.ppermute(value, axis, pairs)


def layer_norm(values):
    average = jnp.mean(values, axis=-1, keepdims=True)
    centred = values - average
    variance = jnp.mean(centred * centred, axis=-1, keepdims=True)
    return centred * lax.rsqrt(variance + epsilon)


def bias_of(rel_bias, first, rows):
    index = np.full((KEYS, rows * PAD), -1, np.int32)
    for kr in range(WIN):
        for kc in range(WIN):
            for qr in range(rows):
                for qc in range(WIN):
                    index[kr * PAD + kc, qr * PAD + qc] = (qr + first - kr + WIN - 1) * (2 * WIN - 1) + (qc - kc + WIN - 1)
    chosen = jnp.asarray(index)[:, None, :] == jnp.arange(rel_bias.shape[0], dtype=jnp.int32)[None, :, None]
    table = jnp.einsum("kpq,ph->khq", chosen.astype(F32), rel_bias, precision=lax.Precision.HIGHEST)
    return table.reshape(KEYS, HEADS * rows * PAD)


def slots(ids):
    count = ids.shape[0]
    wide = jnp.pad(ids.reshape(count, WIN, WIN), ((0, 0), (0, 0), (0, PAD - WIN)), constant_values=-1)
    return wide.reshape(count, KEYS)


def query_slots(ids, first, rows):
    return jnp.concatenate([ids[:, first * PAD : (first + rows) * PAD]] * HEADS, axis=1)


def attend(tokens, att, att_row, base, first, rows, ids_k, ids_q, wqkv, wproj, bias, groups):
    count = rows * PAD
    width = wproj.shape[0]
    head_dim = width // HEADS
    scale = head_dim ** (-0.5)
    lane = lax.broadcasted_iota(jnp.int32, (count, width), 1) // head_dim
    blank = jnp.zeros((PAD, width), F32)

    def group(g, carry):
        tiles = []
        for w in range(GROUP):
            at = (g * GROUP + w) * WIN + PAD - KEEP
            for r in range(WIN):
                tiles.append(tokens[base + r, pl.ds(at, PAD), :])
            tiles.append(blank)
        windows = jnp.concatenate(tiles, axis=0).astype(BF16)
        qkv = jnp.dot(windows, wqkv[...], preferred_element_type=F32)
        queries = qkv[:, :width]
        keys = qkv[:, LANES : LANES + width].astype(BF16)
        values = qkv[:, 2 * LANES : 2 * LANES + width].astype(BF16)
        key_ids = ids_k[g].T
        query_ids = ids_q[g]
        stride = (WIN + 1) * PAD
        contexts = []
        for w in range(GROUP):
            top = w * stride
            own = queries[top + first * PAD : top + first * PAD + count]
            split = jnp.concatenate([jnp.where(lane == h, own, 0.0) for h in range(HEADS)], axis=0).astype(BF16)
            scores = lax.dot_general(
                keys[top : top + KEYS], split, (((1,), (1,)), ((), ())), preferred_element_type=F32
            )
            scores = scores * scale + bias[...]
            scores = jnp.where(key_ids[:KEYS, w : w + 1] == query_ids[w : w + 1, :], scores, NEG)
            scores = jnp.exp(scores - jnp.max(scores, axis=0, keepdims=True))
            weights = (scores / jnp.sum(scores, axis=0, keepdims=True)).astype(BF16)
            mixed = lax.dot_general(
                weights, values[top : top + KEYS], (((0,), (0,)), ((), ())), preferred_element_type=F32
            )
            context = mixed[:count]
            for h in range(1, HEADS):
                context = jnp.where(lane == h, mixed[h * count : (h + 1) * count], context)
            contexts.append(context)
        context = jnp.concatenate(contexts, axis=0).astype(BF16)
        branch = jnp.dot(context, wproj[...], preferred_element_type=F32).astype(BF16).astype(F32)
        for w in range(GROUP):
            at = (g * GROUP + w) * WIN + PAD - KEEP
            for r in range(rows):
                top = w * count + r * PAD
                att[att_row + r, pl.ds(at, PAD), :] = branch[top : top + PAD]
        return carry

    lax.fori_loop(0, groups, group, 0)


def block_kernel(own, before, after, left, right, idk_a, idq_a, idk_b, idq_b, wqkv, wproj, bias_a, bias_b, fc1, fc2, out, tokens, att):
    tile_rows, tile_cols, width = own.shape
    total = 2 * WIN

    def normed(values):
        return layer_norm(values.astype(F32)).astype(BF16).astype(F32)

    for r in range(total):
        if r < KEEP:
            source = before[r]
        elif r < KEEP + WIN:
            source = own[r - KEEP]
        else:
            source = after[r - KEEP - WIN]
        tokens[r, PAD : PAD + tile_cols, :] = normed(source)
    tokens[:, PAD - KEEP : PAD, :] = normed(left[...])
    tail = jnp.concatenate([normed(right[...]), jnp.zeros((total, PAD - SHIFT, width), F32)], axis=1)
    tokens[:, PAD + tile_cols : 2 * PAD + tile_cols, :] = tail
    groups = idk_a.shape[0]
    attend(tokens, att, 0, 0, KEEP, SHIFT, idk_b, idq_b, wqkv, wproj, bias_b, groups)
    attend(tokens, att, SHIFT, WIN, 0, KEEP, idk_a, idq_a, wqkv, wproj, bias_a, groups)

    def row(r, carry):
        summed = own[r].astype(F32) + att[r, PAD : PAD + tile_cols, :]
        second = layer_norm(summed).astype(BF16)
        hidden = jnp.dot(second, fc1[...], preferred_element_type=F32)
        hidden = (0.5 * hidden * (1.0 + lax.erf(hidden * (0.5**0.5)))).astype(BF16)
        out[r] = (summed + jnp.dot(hidden, fc2[...], preferred_element_type=F32)).astype(BF16)
        return carry

    lax.fori_loop(0, tile_rows, row, 0)


def shards(features, region_ids, qkv_weight, proj_weight, rel_bias, fc1_weight, fc2_weight):
    tile_rows, tile_cols, width = features.shape
    before = moved(features[SHIFT:], "row", 1)
    ids_before = moved(region_ids, "row", 1)
    after = moved(features[:SHIFT], "row", -1)
    tall = jnp.concatenate([before, features, after], axis=0)
    left = moved(tall[:, -KEEP:], "col", 1)
    right = moved(tall[:, :SHIFT], "col", -1)
    ids = jnp.concatenate([ids_before, region_ids], axis=0)
    ids = jnp.concatenate([moved(ids[:, -1:], "col", 1), ids], axis=1)
    windows = ids.shape[1]
    groups = -(-windows // GROUP)
    ids = slots(ids.reshape(2 * windows, -1)).reshape(2, groups, GROUP, KEYS)
    ids = jnp.pad(ids, ((0, 0), (0, 0), (0, PAD - GROUP), (0, 0)))
    idk_b, idk_a = ids[0], ids[1]
    idq_b = query_slots(idk_b.reshape(-1, KEYS), KEEP, SHIFT).reshape(groups, PAD, -1)
    idq_a = query_slots(idk_a.reshape(-1, KEYS), 0, KEEP).reshape(groups, PAD, -1)
    wqkv = jnp.pad(qkv_weight.reshape(width, 3, width), ((0, 0), (0, 0), (0, LANES - width))).reshape(width, 3 * LANES)
    bias_a = bias_of(rel_bias, 0, KEEP)
    bias_b = bias_of(rel_bias, KEEP, SHIFT)
    return pl.pallas_call(
        block_kernel,
        out_shape=jax.ShapeDtypeStruct(features.shape, BF16),
        scratch_shapes=[
            pltpu.VMEM((2 * WIN, tile_cols + 2 * PAD, width), F32),
            pltpu.VMEM((tile_rows, tile_cols + 2 * PAD, width), F32),
        ],
        compiler_params=pltpu.CompilerParams(vmem_limit_bytes=48 * 1024 * 1024),
    )(features, before, after, left, right, idk_a, idq_a, idk_b, idq_b, wqkv, proj_weight, bias_a, bias_b, fc1_weight, fc2_weight)


def solution(mesh):
    spec = P(("slide", "row"), "col", None)
    return jax.shard_map(
        shards,
        mesh=mesh,
        in_specs=(spec, spec, P(), P(), P(), P(), P()),
        out_specs=spec,
        check_vma=False,
    )
```

time: 125 us -> 113 us (0.904)
  Pallas kernels: 0 us -> 42.1 us
  local copies, waits for them, and re-layouts: 29.6 us -> 5.14 us
  matrix products: 23.9 us -> 3.83 us
  other arithmetic: 7.66 us -> 0.57 us
  waiting for transfers between devices: 12.8 us -> 7.91 us
  starting transfers between devices: 50.3 us -> 52.6 us
    pallas_call x0 -> x1, Pallas kernels: none -> 42.1 us  [shards(): pl.pallas_call(block_kernel, out_shape=jax.ShapeDtypeStruct(features.shap...]
    reshape x11 -> x3, local copies, waits for them, and re-layouts: 22.6 us -> 0.28 us  [the longest x2 0.16 us: bias_of(): return table.reshape(KEYS, HEADS * rows * PAD)]
    dot_general x6 -> x2, matrix products: 23.9 us -> 3.83 us  [bias_of(): jnp.einsum('kpq,ph->khq', chosen.astype(F32), rel_bias, precision=lax.Pre...]
    ppermute x4 -> x6, waiting for transfers between devices: 12.8 us -> 7.91 us  [moved(): return lax.ppermute(value, axis, pairs)]
    reduce_sum x4 -> x0, other arithmetic: 2.88 us -> none  [the longest x2 1.97 us: layer_norm(): variance = jnp.mean(centred * centred, axis=-1, keepdims=True)]
    slice x6 -> x3, local copies, waits for them, and re-layouts: 3.75 us -> 0.9 us  [the longest x1 0.8 us: shards(): before = moved(features[SHIFT:], 'row', 1)]
    ppermute x4 -> x6, starting transfers between devices: 50.3 us -> 52.6 us  [moved(): return lax.ppermute(value, axis, pairs)]
    sub x1 -> x0, other arithmetic: 2.14 us -> none  [window_attention(): weights = jax.nn.softmax(scores, axis=-1).astype(jnp.bfloat16)]
  transfers between devices with their start and end apart: 4 -> 6, of which waited for: 3 -> 2; matrix products, arithmetic and copies ran while one was open for 5% -> 7% of each run, Pallas kernels for 0% -> 0%
where the time goes in v1:
time: 113 us; the launch traced here: 112 us
  starting transfers between devices  52.6 us (47%)
  Pallas kernels  42.1 us (37%)
  waiting for transfers between devices  7.91 us (7%)
  local copies, waits for them, and re-layouts  5.14 us (5%)
  matrix products  3.83 us (3%)
    ppermute x6, starting transfers between devices, moved(): return lax.ppermute(value, axis, pairs)  52.6 us
    pallas_call x1, Pallas kernels, shards(): pl.pallas_call(block_kernel, out_shape=jax.ShapeDtypeStruct(features.shap...  42.1 us
    ppermute x6, waiting for transfers between devices, moved(): return lax.ppermute(value, axis, pairs)  7.91 us
    dot_general x2, matrix products, bias_of(): jnp.einsum('kpq,ph->khq', chosen.astype(F32), rel_bias, precision=lax.Pre...  3.83 us
  transfers between devices with their start and end apart: 6, of which 2 were waited for; matrix products, arithmetic and copies ran while one was open for 7% of the time, Pallas kernels for 0%

profile of v1, /device:TPU:40, one launch (start us, length us, event | category | flops | bytes accessed | tf_op | source)
XLA Modules:
  0.0 112.4 jit_solution(8439937048519242005)
XLA Ops:
  0.0 1.5 %copy.25.own = bf16[7,448,96]{2,1,0:T(8,128)(2,1)S(1)} copy(bf16[7,448,96]{1,2,0:T(8,128)(2,1)} %param.9) | data formatting | bytes 1204224 | tf_op args[0]
  1.6 43.0 %collective-permute-start.1 = (bf16[3,448,96]{2,1,0:T(8,128)(2,1)S(1)}, bf16[3,448,96]{2,1,0:T(8,128)(2,1)S(1)}, u32[]{:S(2)}, u32[]{:S(2)}) collective-permute-start(bf16[3,448,96]{2,1,0:T(8,128)(2,1)S(1)} %slice.37), channel_id=1, source_target_pairs={{0,252},{4,0},{8,4},{12,8},{16,12},{20,16},{24,20},{28,24},{32,28}... | collective-permute-start | bytes 774152 | tf_op jit(solution)/shard_map/ppermute | solution.py:29
  44.6 0.8 slice.36
  45.4 2.0 %fusion.3 = f32[56,3,32]{2,1,0:T(4,128)S(1)} fusion(s32[56,32]{1,0:T(8,128)S(1)} %copy-done.6, f32[169,3]{0,1:T(4,128)S(1)} %copy-done), kind=kOutput, calls=%fused_computation.5 | convolution fusion | flops 11205376 | bytes 30700 | tf_op jit(solution)/shard_map/kpq,ph->khq/dot_general | solution.py:47
  47.4 1.9 %fusion.2 = f32[56,3,24]{2,1,0:T(4,128)S(1)} fusion(s32[56,24]{1,0:T(8,128)S(1)} %copy-done.7, f32[169,3]{0,1:T(4,128)S(1)} %copy-done), kind=kOutput, calls=%fused_computation.4 | convolution fusion | flops 8404032 | bytes 23532 | tf_op jit(solution)/shard_map/kpq,ph->khq/dot_general | solution.py:47
  49.2 0.1 copy.21
  49.4 0.1 copy.30.wqkv
  49.5 0.2 pad_add_fusion
  49.7 3.6 %collective-permute-start.5 = (s32[2,1,49]{1,0,2:T(2,128)S(1)}, s32[2,1,49]{1,0,2:T(2,128)S(1)}, u32[]{:S(2)}, u32[]{:S(2)}) collective-permute-start(s32[2,1,49]{1,0,2:T(2,128)S(1)} %pad_add_fusion), channel_id=1, source_target_pairs={{0,1},{1,2},{2,3},{3,0},{4,5},{5,6},{6,7},{7,4},{8,9},{9,10},{10,1... | collective-permute-start | bytes 1184 | tf_op jit(solution)/shard_map/ppermute | solution.py:29
  53.3 0.1 copy.28.fc2
  53.6 0.1 copy.24
  53.7 0.1 copy.27.bias_b
  53.8 3.2 %collective-permute-done.5 = s32[2,1,49]{1,0,2:T(2,128)S(1)} collective-permute-done((s32[2,1,49]{1,0,2:T(2,128)S(1)}, s32[2,1,49]{1,0,2:T(2,128)S(1)}, u32[]{:S(2)}, u32[]{:S(2)}) %collective-permute-start.5) | collective-permute-done | bytes 424 | tf_op jit(solution)/shard_map/ppermute | solution.py:29
  57.0 0.2 add_add_fusion
  57.1 0.1 reshape_reshape.6
  57.2 0.4 copy.20
  57.7 0.2 reshape_reshape.7
  58.0 0.1 add_bitcast_fusion.1.idq_b
  58.2 4.0 %collective-permute-start.3 = (bf16[14,3,96]{2,1,0:T(4,128)(2,1)S(1)}, bf16[14,3,96]{2,1,0:T(4,128)(2,1)S(1)}, u32[]{:S(2)}, u32[]{:S(2)}) collective-permute-start(bf16[14,3,96]{2,1,0:T(4,128)(2,1)S(1)} %pad_maximum_fusion), channel_id=1, source_target_pairs={{0,3},{1,0},{2,1},{3,2},{4,7},{5,4},{6,5},{7,6},{8,11},{9,8},{10,9... | collective-permute-start | bytes 24200 | tf_op jit(solution)/shard_map/ppermute | solution.py:29
  62.2 2.0 %collective-permute-start.2 = (bf16[14,4,96]{2,1,0:T(4,128)(2,1)S(1)}, bf16[14,4,96]{2,1,0:T(4,128)(2,1)S(1)}, u32[]{:S(2)}, u32[]{:S(2)}) collective-permute-start(bf16[14,4,96]{2,1,0:T(4,128)(2,1)S(1)} %pad_maximum_fusion.2), channel_id=1, source_target_pairs={{0,1},{1,2},{2,3},{3,0},{4,5},{5,6},{6,7},{7,4},{8,9},{9,10},{10,1... | collective-permute-start | bytes 32264 | tf_op jit(solution)/shard_map/ppermute | solution.py:29
  64.2 0.1 add_bitcast_fusion.idq_a
  64.3 4.7 %collective-permute-done.2.left = bf16[14,4,96]{2,1,0:T(4,128)(2,1)S(1)} collective-permute-done((bf16[14,4,96]{2,1,0:T(4,128)(2,1)S(1)}, bf16[14,4,96]{2,1,0:T(4,128)(2,1)S(1)}, u32[]{:S(2)}, u32[]{:S(2)}) %collective-permute-start.2) | collective-permute-done | bytes 10784 | tf_op jit(solution)/shard_map/ppermute | solution.py:29
  69.1 42.1 %shard_map.91 = bf16[7,448,96]{2,1,0:T(8,128)(2,1)S(1)} custom-call(bf16[7,448,96]{2,1,0:T(8,128)(2,1)S(1)} %copy.25.own, bf16[4,448,96]{2,1,0:T(8,128)(2,1)S(1)} %collective-permute-done.before, bf16[3,448,96]{2,1,0:T(8,128)(2,1)S(1)} %collective-permute-done.1.after, bf16[14,4,96]{2,1,0:T(4,128)(2,1)S(1)} %collective-permute-done.2.left, ...), custom_call_target="tpu_custom_call" | custom-call | tf_op jit(solution)/shard_map/pallas_call | solution.py:168
  111.2 1.2 %copy.29 = bf16[7,448,96]{1,2,0:T(8,128)(2,1)} copy(bf16[7,448,96]{2,1,0:T(8,128)(2,1)S(1)} %shard_map.91) | data formatting | bytes 1204224 | tf_op jit(solution)/shard_map/pallas_call | solution.py:168
  (31 shorter events, 0.4 us)
Async XLA Ops:
  0.0 45.4 %copy-start = (f32[169,3]{0,1:T(4,128)S(1)}, f32[169,3]{0,1:T(4,128)}, u32[]{:S(2)}) copy-start(f32[169,3]{0,1:T(4,128)} %param.13) | copy-start | bytes 6088
  0.0 49.5 %collective-permute-start.4 = (s32[1,64,49]{1,0,2:T(1,128)}, s32[1,64,49]{1,0,2:T(1,128)S(1)}, u32[]{:S(2)}, u32[]{:S(2)}) collective-permute-start(s32[1,64,49]{1,0,2:T(1,128)} %param.10), channel_id=1, source_target_pairs={{0,4},{4,8},{8,12},{12,16},{16,20},{20,24},{24,28},{28,32},{32,36}... | collective-permute-start | bytes 37640 | tf_op jit(solution)/shard_map/ppermute | solution.py:29
  1.6 43.8 %copy-start.6 = (s32[56,32]{1,0:T(8,128)S(1)}, s32[56,32]{1,0:T(8,128)}, u32[]{:S(2)}) copy-start(s32[56,32]{1,0:T(8,128)} %constant.10.clone) | copy-start | bytes 21508
  1.6 45.8 %copy-start.7 = (s32[56,24]{1,0:T(8,128)S(1)}, s32[56,24]{1,0:T(8,128)}, u32[]{:S(2)}) copy-start(s32[56,24]{1,0:T(8,128)} %constant.11.clone) | copy-start | bytes 16132
  1.6 47.6 %copy-start.4 = (bf16[96,288]{1,0:T(8,128)(2,1)S(1)}, bf16[96,288]{1,0:T(8,128)(2,1)}, u32[]{:S(2)}) copy-start(bf16[96,288]{1,0:T(8,128)(2,1)} %param.11) | copy-start | bytes 165892
  1.6 56.5 %collective-permute-start.1 = (bf16[3,448,96]{2,1,0:T(8,128)(2,1)S(1)}, bf16[3,448,96]{2,1,0:T(8,128)(2,1)S(1)}, u32[]{:S(2)}, u32[]{:S(2)}) collective-permute-start(bf16[3,448,96]{2,1,0:T(8,128)(2,1)S(1)} %slice.37), channel_id=1, source_target_pairs={{0,252},{4,0},{8,4},{12,8},{16,12},{20,16},{24,20},{28,24},{32,28}... | collective-permute-start | bytes 774152 | tf_op jit(solution)/shard_map/ppermute | solution.py:29
  45.4 4.2 %copy-start.3 = (s32[1,64,49]{1,0,2:T(1,128)S(1)}, s32[1,64,49]{1,0,2:T(1,128)}, u32[]{:S(2)}) copy-start(s32[1,64,49]{1,0,2:T(1,128)} %param.10) | copy-start | bytes 37636
  45.4 7.9 %copy-start.5 = (bf16[384,96]{0,1:T(8,128)(2,1)S(1)}, bf16[384,96]{0,1:T(8,128)(2,1)}, u32[]{:S(2)}) copy-start(bf16[384,96]{0,1:T(8,128)(2,1)} %param.15) | copy-start | bytes 221188
  45.4 12.7 %collective-permute-start = (bf16[4,448,96]{2,1,0:T(8,128)(2,1)}, bf16[4,448,96]{2,1,0:T(8,128)(2,1)S(1)}, u32[]{:S(2)}, u32[]{:S(2)}) collective-permute-start(bf16[4,448,96]{2,1,0:T(8,128)(2,1)} %slice.36), channel_id=1, source_target_pairs={{0,4},{4,8},{8,12},{12,16},{16,20},{20,24},{24,28},{28,32},{32,36}... | collective-permute-start | bytes 1032200 | tf_op jit(solution)/shard_map/ppermute | solution.py:29
  49.7 7.2 %collective-permute-start.5 = (s32[2,1,49]{1,0,2:T(2,128)S(1)}, s32[2,1,49]{1,0,2:T(2,128)S(1)}, u32[]{:S(2)}, u32[]{:S(2)}) collective-permute-start(s32[2,1,49]{1,0,2:T(2,128)S(1)} %pad_add_fusion), channel_id=1, source_target_pairs={{0,1},{1,2},{2,3},{3,0},{4,5},{5,6},{6,7},{7,4},{8,9},{9,10},{10,1... | collective-permute-start | bytes 1184 | tf_op jit(solution)/shard_map/ppermute | solution.py:29
  58.1 10.9 %copy-start.1 = (bf16[96,384]{1,0:T(8,128)(2,1)S(1)}, bf16[96,384]{1,0:T(8,128)(2,1)}, u32[]{:S(2)}) copy-start(bf16[96,384]{1,0:T(8,128)(2,1)} %fc1.1) | copy-start | bytes 221188
  58.1 10.9 %copy-start.2 = (bf16[96,96]{1,0:T(8,128)(2,1)S(1)}, bf16[96,96]{1,0:T(8,128)(2,1)}, u32[]{:S(2)}) copy-start(bf16[96,96]{1,0:T(8,128)(2,1)} %wproj.1) | copy-start | bytes 55300
  58.2 6.2 %collective-permute-start.3 = (bf16[14,3,96]{2,1,0:T(4,128)(2,1)S(1)}, bf16[14,3,96]{2,1,0:T(4,128)(2,1)S(1)}, u32[]{:S(2)}, u32[]{:S(2)}) collective-permute-start(bf16[14,3,96]{2,1,0:T(4,128)(2,1)S(1)} %pad_maximum_fusion), channel_id=1, source_target_pairs={{0,3},{1,0},{2,1},{3,2},{4,7},{5,4},{6,5},{7,6},{8,11},{9,8},{10,9... | collective-permute-start | bytes 24200 | tf_op jit(solution)/shard_map/ppermute | solution.py:29
  62.2 6.9 %collective-permute-start.2 = (bf16[14,4,96]{2,1,0:T(4,128)(2,1)S(1)}, bf16[14,4,96]{2,1,0:T(4,128)(2,1)S(1)}, u32[]{:S(2)}, u32[]{:S(2)}) collective-permute-start(bf16[14,4,96]{2,1,0:T(4,128)(2,1)S(1)} %pad_maximum_fusion.2), channel_id=1, source_target_pairs={{0,1},{1,2},{2,3},{3,0},{4,5},{5,6},{6,7},{7,4},{8,9},{9,10},{10,1... | collective-permute-start | bytes 32264 | tf_op jit(solution)/shard_map/ppermute | solution.py:29
